TPU v7x, 256 devices: a whole 4x4x8 slice. The times are simulated.
256 devices in a mesh: gx: 16 (over y_hi, z), gy: 4 (over x), gz: 4 (over y_lo, core).
Axes of the slice: x: 4, y: 4 (y_hi: 2, y_lo: 2; y = y_hi * 2 + y_lo), z: 8, core: 2. Of those that a mesh axis runs over, the one named last changes fastest.
Arguments:
- fields: float32 [4, 64, 256, 512], P(None, 'gx', 'gy', 'gz'), may hold values from -8 to 8
- volume_code: int32 [64, 256, 512], P('gx', 'gy', 'gz'), may hold values from 65536 to 1048576
- cut_flag: int32 [64, 256, 512], P('gx', 'gy', 'gz'), may hold values 0 or 1
- member_bits: int32 [64, 256, 512], P('gx', 'gy', 'gz'), may hold values from 0 to 134217727
Outputs:
- merged: float32 [4, 64, 256, 512], P(None, 'gx', 'gy', 'gz')
All inputs are finite; a program needn't handle non-finite values. No bound on the sum of `cut_flag` on one device may be relied on, other than what follows from the above.
Results may differ from a plain program's by a relative error of at most 0.00015.
Values sent between devices are 32-bit elements; how exact they have to be, the bound alone decides.
A program may use at most 128 MiB of HBM per device.

v0:
```python
import jax
import jax.numpy as jnp
from jax import lax
from jax.experimental import pallas as pl
from jax.experimental.pallas import tpu as pltpu
from jax.sharding import PartitionSpec as P

MESH = pl.DeviceIdType.MESH
FIELDS = 4
LAYERS = 4
ROWS = 64
TILES = ROWS // 8
PADDED = ROWS + 16
LANES = 128
SIGNS = (-1, 1)

TRAVEL = []
for kind in ((1, 0, 0), (1, 1, 0), (1, 0, 1), (1, 1, 1), (0, 0, 1), (0, 1, 0), (0, 1, 1)):
    for sx in SIGNS if kind[0] else (0,):
        for sy in SIGNS if kind[1] else (0,):
            for sz in SIGNS if kind[2] else (0,):
                TRAVEL.append((sx, sy, sz))


def side(sign):
    return (sign + 1) // 2


def offset_bit(dx, dy, dz):
    return 9 * (dx + 1) + 3 * (dy + 1) + (dz + 1)


def neighbour(travel):
    result = {}
    for axis, sign in zip(("gx", "gy", "gz"), travel):
        if sign:
            count = lax.axis_size(axis)
            result[axis] = lax.rem(lax.axis_index(axis) + sign + count, count)
    return result


def turn(value, shift):
    if isinstance(shift, int):
        shift = shift % LANES
        if shift == 0:
            return value
    return pltpu.roll(value, shift, 1)


def kernel(fields, volume_code, cut_flag, member_bits, out, raw, code, cut, bits, act, kap, inv_count,
           inv_volume, w, acc, result, hats, xface, yrows, edges, zpack, xzpack, yzpack, cpack,
           rx, ry, re, rz, rxz, ryz, rc, in_sem, out_sem, send_sem, recv_sem):
    lane8 = lax.broadcasted_iota(jnp.int32, (8, LANES), 1)
    lane1 = lax.broadcasted_iota(jnp.int32, (1, LANES), 1)
    zero8 = jnp.zeros((8, LANES), jnp.float32)

    loads = []
    for index, (source, target) in enumerate(
        ((volume_code, code), (cut_flag, cut), (member_bits, bits), (fields, raw))
    ):
        copy = pltpu.make_async_copy(source, target, in_sem.at[index])
        copy.start()
        loads.append(copy)
    barrier = pltpu.get_barrier_semaphore()
    for travel in TRAVEL:
        pl.semaphore_signal(barrier, inc=1, device_id=neighbour(travel), device_id_type=MESH)

    for x in range(LAYERS):
        for rows in (0, PADDED - 8):
            act[x, rows : rows + 8, :] = jnp.zeros((8, LANES), jnp.int32)
            for f in range(FIELDS + 1):
                w[f, x, rows : rows + 8, :] = zero8
    for copy in loads:
        copy.wait()

    def prepare(t, carry):
        own = pl.ds(pl.multiple_of(8 * t, 8), 8)
        padded = pl.ds(pl.multiple_of(8 * t + 8, 8), 8)
        for x in range(LAYERS):
            kappa = code[x, own, :].astype(jnp.float32) * (1.0 / 1048576.0)
            active = bits[x, own, :] * cut[x, own, :]
            act[x, padded, :] = active
            kap[x, own, :] = kappa
            others = lax.population_count(jnp.bitwise_and(active, ((1 << 27) - 1) ^ (1 << 13)))
            inv_count[x, own, :] = 1.0 / (others + 1).astype(jnp.float32)
            w[FIELDS, x, padded, :] = kappa
            for f in range(FIELDS):
                w[f, x, padded, :] = kappa * raw[f, x, own, :]
        return carry

    lax.fori_loop(0, TILES, prepare, 0)
    pl.semaphore_wait(barrier, len(TRAVEL))

    def message(stage, travel):
        sx, sy, sz = travel
        count = FIELDS + 1 if stage == 0 else FIELDS
        ix, iy, iz = side(sx), side(sy), side(sz)
        e = 2 * ix + iy
        if sx and not sy and not sz:
            if stage % 2 == 0:
                source, target = xface.at[stage // 2, ix, 0:count], rx.at[stage // 2, ix, 0:count]
            else:
                mid = hats.at[stage // 2, 1]
                source = mid.at[:, 4 if sx == 1 else 1, 8 : 8 + ROWS, :]
                target = mid.at[:, 0 if sx == 1 else 5, 8 : 8 + ROWS, :]
        elif sy and not sx and not sz:
            source, target = yrows.at[stage, iy], ry.at[stage, iy]
        elif sz and not sx and not sy:
            source, target = zpack.at[stage], rz.at[stage, iz]
        elif sx and sy and not sz:
            source, target = edges.at[stage, e], re.at[stage, e]
        elif sx and sz and not sy:
            source, target = xzpack.at[stage, ix], rxz.at[stage, ix, iz]
        elif sy and sz and not sx:
            source, target = yzpack.at[stage, iy], ryz.at[stage, iy, iz]
        else:
            source, target = cpack.at[stage, e], rc.at[stage, e, iz]
        index = TRAVEL.index(travel)
        return pltpu.make_async_remote_copy(
            src_ref=source,
            dst_ref=target,
            send_sem=send_sem.at[stage, index],
            recv_sem=recv_sem.at[stage, index],
            device_id=neighbour(travel),
            device_id_type=MESH,
        )

    started = []

    def send(stage, chosen):
        for travel in TRAVEL:
            if chosen(*travel):
                copy = message(stage, travel)
                copy.start()
                started.append(copy)

    def receive(stage, chosen):
        for travel in TRAVEL:
            if chosen(*travel):
                message(stage, travel).wait_recv()

    def pushed(xt, row, dys, count):
        sums = [[None] * count for _ in range(3)]
        for dx in (-1, 0, 1):
            xs = xt - dx
            if xs < 0 or xs >= LAYERS:
                continue
            for dy in dys:
                rows = pl.ds(row - dy, 8)
                active = act[xs, rows, :]
                values = [w[f, xs, rows, :] for f in range(count)]
                for dz in (-1, 0, 1):
                    bit = offset_bit(dx, dy, dz)
                    if bit != 13:
                        chosen = jnp.bitwise_and(active, 1 << bit) != 0
                    for f in range(count):
                        term = values[f] if bit == 13 else jnp.where(chosen, values[f], 0.0)
                        old = sums[dz + 1][f]
                        sums[dz + 1][f] = term if old is None else old + term
        mains, ends = [], []
        for f in range(count):
            up = turn(sums[2][f], 1)
            down = turn(sums[0][f], -1)
            mains.append(
                sums[1][f] + jnp.where(lane8 == 0, 0.0, up) + jnp.where(lane8 == LANES - 1, 0.0, down)
            )
            ends.append(jnp.where(lane8 < LANES // 2, up, down))
        return mains, ends

    def packed(base, value, p, lane):
        return jnp.where(jnp.right_shift(lane, 1) == p, turn(value, 1 + 2 * p), base)

    def scatter(stage, count):
        for sx in SIGNS:
            xt = -1 if sx == -1 else LAYERS
            ix = side(sx)

            def layer(t, pack, xt=xt, ix=ix):
                mains, ends = pushed(xt, 8 * t + 8, (-1, 0, 1), count)
                own = pl.ds(pl.multiple_of(8 * t, 8), 8)
                small = zero8
                for f in range(count):
                    xface[stage // 2, ix, f, own, :] = mains[f]
                    small = packed(small, ends[f], f, lane8)
                start = 2 * count * t
                inside = (lane8 >= start) & (lane8 < start + 2 * count)
                return jnp.where(inside, turn(small, start), pack)

            xzpack[stage, ix] = lax.fori_loop(0, TILES, layer, zero8)
            send(stage, lambda a, b, c: (a, b, c) == (sx, 0, 0))
        for sx in SIGNS:
            xt = -1 if sx == -1 else LAYERS
            for sy in SIGNS:
                mains, ends = pushed(xt, 0 if sy == -1 else PADDED - 8, (sy,), count)
                row = 7 if sy == -1 else 0
                e = 2 * side(sx) + side(sy)
                small = zero8
                for f in range(count):
                    edges[stage, e, f : f + 1, :] = mains[f][row : row + 1, :]
                    small = packed(small, ends[f], f, lane8)
                cpack[stage, e] = small[row : row + 1, :]
        send(stage, lambda a, b, c: a != 0 and (b != 0 or c != 0))

        def rest(t, carry):
            own = pl.ds(pl.multiple_of(8 * t, 8), 8)
            pack = zero8
            for xt in range(LAYERS):
                mains, ends = pushed(xt, 8 * t + 8, (-1, 0, 1), count)
                for f in range(count):
                    acc[f, xt, own, :] = mains[f]
                    pack = packed(pack, ends[f], 4 * f + xt, lane8)
            zpack[stage, t] = pack
            return carry

        lax.fori_loop(0, TILES, rest, 0)
        send(stage, lambda a, b, c: (a, b) == (0, 0))
        for sy in SIGNS:
            row = 7 if sy == -1 else 0
            pack = zero8
            for xt in range(LAYERS):
                mains, ends = pushed(xt, 0 if sy == -1 else PADDED - 8, (sy,), count)
                for f in range(count):
                    p = 4 * f + xt
                    yrows[stage, side(sy), p : p + 1, :] = mains[f][row : row + 1, :]
                    pack = packed(pack, ends[f], p, lane8)
            yzpack[stage, side(sy)] = pack[row : row + 1, :]
        send(stage, lambda a, b, c: a == 0 and b != 0)

    def edge_lanes(value, lane):
        return jnp.where((lane == 0) | (lane == LANES - 1), value, 0.0)

    def merged_pairs(up, down, lane):
        return jnp.where(jnp.bitwise_and(lane, 1) == 1, up, down)

    def combine(stage, count):
        odd = stage + 1
        which = stage // 2
        receive(stage, lambda a, b, c: True)
        for sy in SIGNS:
            iy = side(sy)
            row = 0 if sy == 1 else ROWS - 1
            yz = merged_pairs(ryz[stage, iy, 1], ryz[stage, iy, 0], lane1)
            for x in range(LAYERS):
                sx = 1 if x == 0 else -1 if x == LAYERS - 1 else 0
                if sx:
                    e = 2 * side(sx) + iy
                    corner = merged_pairs(rc[stage, e, 1], rc[stage, e, 0], lane1)
                for f in range(count):
                    p = 4 * f + x
                    value = ry[stage, iy, p : p + 1, :]
                    ends = turn(yz, LANES - 1 - 2 * p)
                    if sx:
                        value = value + re[stage, e, f : f + 1, :]
                        ends = ends + turn(corner, LANES - 1 - 2 * f)
                    acc[f, x, row : row + 1, :] += value + edge_lanes(ends, lane1)

        def group(layers, first):
            def tile(t, packs):
                own = pl.ds(pl.multiple_of(8 * t, 8), 8)
                padded = pl.ds(pl.multiple_of(8 * t + 8, 8), 8)
                z = merged_pairs(rz[stage, 1, t], rz[stage, 0, t], lane8)
                pack = zero8 if first else zpack[odd, t]
                packs = list(packs)
                for x in layers:
                    sx = 1 if x == 0 else -1 if x == LAYERS - 1 else 0
                    if sx:
                        xz = merged_pairs(rxz[stage, side(sx), 1], rxz[stage, side(sx), 0], lane8)
                        xz = turn(xz, LANES - 1 - 2 * count * t)
                    sums = []
                    for f in range(count):
                        value = acc[f, x, own, :]
                        ends = turn(z, LANES - 1 - 2 * (4 * f + x))
                        if sx:
                            value = value + rx[which, side(sx), f, own, :]
                            ends = ends + turn(xz, -2 * f)
                        sums.append(value + edge_lanes(ends, lane8))
                    if stage == 0:
                        inverse = 1.0 / sums[FIELDS]
                        inv_volume[x, own, :] = inverse
                    else:
                        inverse = inv_volume[x, own, :]
                    small = zero8
                    for f in range(FIELDS):
                        hat = sums[f] * inverse
                        hats[which, 1, f, x + 1, padded, :] = hat
                        pack = packed(pack, hat, 4 * f + x, lane8)
                        if sx:
                            small = packed(small, hat, f, lane8)
                    if sx:
                        start = 2 * FIELDS * t
                        inside = (lane8 >= start) & (lane8 < start + 2 * FIELDS)
                        slot = side(-sx)
                        packs[slot] = jnp.where(inside, turn(small, start), packs[slot])
                zpack[odd, t] = pack
                return tuple(packs)

            return lax.fori_loop(0, TILES, tile, (zero8, zero8))

        packs = group((0, LAYERS - 1), True)
        send(odd, lambda a, b, c: a != 0 and b == 0 and c == 0)
        for sx in SIGNS:
            xzpack[odd, side(sx)] = packs[side(sx)]
            x = 0 if sx == -1 else LAYERS - 1
            for sy in SIGNS:
                row = 8 if sy == -1 else 7 + ROWS
                e = 2 * side(sx) + side(sy)
                small = jnp.zeros((1, LANES), jnp.float32)
                for f in range(FIELDS):
                    value = hats[which, 1, f, x + 1, row : row + 1, :]
                    edges[odd, e, f : f + 1, :] = value
                    small = packed(small, value, f, lane1)
                cpack[odd, e] = small
        send(odd, lambda a, b, c: a != 0 and (b != 0 or c != 0))
        group(tuple(range(1, LAYERS - 1)), False)
        send(odd, lambda a, b, c: (a, b) == (0, 0))
        for sy in SIGNS:
            row = 8 if sy == -1 else 7 + ROWS
            for x in range(LAYERS):
                for f in range(FIELDS):
                    p = 4 * f + x
                    yrows[odd, side(sy), p : p + 1, :] = hats[which, 1, f, x + 1, row : row + 1, :]
            t = 0 if sy == -1 else TILES - 1
            yzpack[odd, side(sy)] = zpack[odd, t, row % 8 : row % 8 + 1, :]
        send(odd, lambda a, b, c: a == 0 and b != 0)

    def swapped_pairs(from_below, from_above, lane):
        return jnp.where(jnp.bitwise_and(lane, 1) == 1, turn(from_below, 1), turn(from_above, -1))

    def store_shifted(which, f, xi, rows, value, ends, lane):
        hats[which, 2, f, xi, rows, :] = jnp.where(lane == LANES - 1, ends, turn(value, -1))
        hats[which, 0, f, xi, rows, :] = jnp.where(lane == 0, ends, turn(value, 1))

    def gather(stage, last):
        which = stage // 2
        receive(stage, lambda a, b, c: True)
        for sy in SIGNS:
            iy = side(sy)
            row = 7 if sy == 1 else 8 + ROWS
            rows = slice(row, row + 1)
            yz = swapped_pairs(ryz[stage, iy, 1], ryz[stage, iy, 0], lane1)
            for x in range(-1, LAYERS + 1):
                sx = 1 if x == -1 else -1 if x == LAYERS else 0
                if sx:
                    e = 2 * side(sx) + iy
                    corner = swapped_pairs(rc[stage, e, 1], rc[stage, e, 0], lane1)
                for f in range(FIELDS):
                    p = 4 * f + x
                    if sx:
                        value = re[stage, e, f : f + 1, :]
                        ends = turn(corner, LANES - 1 - 2 * f)
                    else:
                        value = ry[stage, iy, p : p + 1, :]
                        ends = turn(yz, LANES - 1 - 2 * p)
                    hats[which, 1, f, x + 1, rows, :] = value
                    store_shifted(which, f, x + 1, rows, value, ends, lane1)

        def shifts(t, carry):
            padded = pl.ds(pl.multiple_of(8 * t + 8, 8), 8)
            z = swapped_pairs(rz[stage, 1, t], rz[stage, 0, t], lane8)
            for x in range(-1, LAYERS + 1):
                sx = 1 if x == -1 else -1 if x == LAYERS else 0
                if sx:
                    xz = swapped_pairs(rxz[stage, side(sx), 1], rxz[stage, side(sx), 0], lane8)
                    xz = turn(xz, LANES - 1 - 2 * FIELDS * t)
                for f in range(FIELDS):
                    ends = turn(xz, -2 * f) if sx else turn(z, LANES - 1 - 2 * (4 * f + x))
                    value = hats[which, 1, f, x + 1, padded, :]
                    store_shifted(which, f, x + 1, padded, value, ends, lane8)
            return carry

        lax.fori_loop(0, TILES, shifts, 0)

        def tile(t, carry):
            own = pl.ds(pl.multiple_of(8 * t, 8), 8)
            padded = pl.ds(pl.multiple_of(8 * t + 8, 8), 8)
            for x in range(LAYERS):
                active = act[x, padded, :]
                sums = [hats[which, 1, f, x + 1, padded, :] for f in range(FIELDS)]
                for dx in (-1, 0, 1):
                    for dy in (-1, 0, 1):
                        for dz in (-1, 0, 1):
                            bit = offset_bit(dx, dy, dz)
                            if bit == 13:
                                continue
                            chosen = jnp.bitwise_and(active, 1 << bit) != 0
                            rows = pl.ds(8 * t + 8 + dy, 8)
                            for f in range(FIELDS):
                                value = hats[which, dz + 1, f, x + 1 + dx, rows, :]
                                sums[f] = sums[f] + jnp.where(chosen, value, 0.0)
                scale = inv_count[x, own, :]
                if not last:
                    scale = scale * kap[x, own, :]
                for f in range(FIELDS):
                    if last:
                        result[f, x, own, :] = sums[f] * scale
                    else:
                        w[f, x, padded, :] = sums[f] * scale
            return carry

        lax.fori_loop(0, TILES, tile, 0)

    scatter(0, FIELDS + 1)
    combine(0, FIELDS + 1)
    gather(1, False)
    scatter(2, FIELDS)
    combine(2, FIELDS)
    gather(3, True)
    copy = pltpu.make_async_copy(result, out, out_sem)
    copy.start()
    for sent in started:
        sent.wait_send()
    copy.wait()


def body(fields, volume_code, cut_flag, member_bits):
    f32, i32 = jnp.float32, jnp.int32
    vmem = pltpu.VMEM
    block = (LAYERS, ROWS, LANES)
    padded = (LAYERS, PADDED, LANES)
    row_count = 24
    scratch = [
        vmem((FIELDS,) + block, f32),
        vmem(block, i32),
        vmem(block, i32),
        vmem(block, i32),
        vmem(padded, i32),
        vmem(block, f32),
        vmem(block, f32),
        vmem(block, f32),
        vmem((FIELDS + 1,) + padded, f32),
        vmem((FIELDS + 1,) + block, f32),
        vmem((FIELDS,) + block, f32),
        vmem((2, 3, FIELDS, LAYERS + 2, PADDED, LANES), f32),
        vmem((2, 2, FIELDS + 1, ROWS, LANES), f32),
        vmem((4, 2, row_count, LANES), f32),
        vmem((4, 4, 8, LANES), f32),
        vmem((4, TILES, 8, LANES), f32),
        vmem((4, 2, 8, LANES), f32),
        vmem((4, 2, 1, LANES), f32),
        vmem((4, 4, 1, LANES), f32),
        vmem((2, 2, FIELDS + 1, ROWS, LANES), f32),
        vmem((4, 2, row_count, LANES), f32),
        vmem((4, 4, 8, LANES), f32),
        vmem((4, 2, TILES, 8, LANES), f32),
        vmem((4, 2, 2, 8, LANES), f32),
        vmem((4, 2, 2, 1, LANES), f32),
        vmem((4, 4, 2, 1, LANES), f32),
        pltpu.SemaphoreType.DMA((4,)),
        pltpu.SemaphoreType.DMA,
        pltpu.SemaphoreType.DMA((4, len(TRAVEL))),
        pltpu.SemaphoreType.DMA((4, len(TRAVEL))),
    ]
    anywhere = pl.BlockSpec(memory_space=pl.ANY)
    return pl.pallas_call(
        kernel,
        out_shape=jax.ShapeDtypeStruct((FIELDS,) + block, f32),
        in_specs=[anywhere] * 4,
        out_specs=anywhere,
        scratch_shapes=scratch,
        compiler_params=pltpu.CompilerParams(
            collective_id=0, has_side_effects=True, vmem_limit_bytes=48 * 1024 * 1024
        ),
    )(fields, volume_code, cut_flag, member_bits)


def solution(mesh):
    in_specs = (
        P(None, "gx", "gy", "gz"),
        P("gx", "gy", "gz"),
        P("gx", "gy", "gz"),
        P("gx", "gy", "gz"),
    )
    out_specs = P(None, "gx", "gy", "gz")
    return jax.shard_map(body, mesh=mesh, in_specs=in_specs, out_specs=out_specs, check_vma=False)
```

profile of v0, /device:TPU:1, one launch (start us, length us, event | category | flops | bytes accessed | tf_op | source)
XLA Modules:
  0.0 66.9 jit_solution(17770270436102080861)
XLA Ops:
  0.0 0.0 copy-start
  0.0 1.0 %copy-done = f32[4,4,64,128]{3,2,1,0:T(8,128)S(1)} copy-done((f32[4,4,64,128]{3,2,1,0:T(8,128)S(1)}, f32[4,4,64,128]{3,2,1,0:T(8,128)}, u32[]{:S(2)}) %copy-start) | copy-done | bytes 524312
  1.0 0.0 copy-start.1
  1.0 0.9 %copy-done.1 = s32[4,64,128]{2,1,0:T(8,128)S(1)} copy-done((s32[4,64,128]{2,1,0:T(8,128)S(1)}, s32[4,64,128]{2,1,0:T(8,128)}, u32[]{:S(2)}) %copy-start.1) | copy-done | bytes 131096
  1.9 0.0 copy-start.2
  1.9 0.9 %copy-done.2 = s32[4,64,128]{2,1,0:T(8,128)S(1)} copy-done((s32[4,64,128]{2,1,0:T(8,128)S(1)}, s32[4,64,128]{2,1,0:T(8,128)}, u32[]{:S(2)}) %copy-start.2) | copy-done | bytes 131096
  2.9 0.0 copy-start.3
  2.9 0.9 %copy-done.3 = s32[4,64,128]{2,1,0:T(8,128)S(1)} copy-done((s32[4,64,128]{2,1,0:T(8,128)S(1)}, s32[4,64,128]{2,1,0:T(8,128)}, u32[]{:S(2)}) %copy-start.3) | copy-done | bytes 131096
  3.8 62.4 %shard_map.46 = f32[4,4,64,128]{3,2,1,0:T(8,128)S(1)} custom-call(f32[4,4,64,128]{3,2,1,0:T(8,128)S(1)} %copy-done, s32[4,64,128]{2,1,0:T(8,128)S(1)} %copy-done.1, s32[4,64,128]{2,1,0:T(8,128)S(1)} %copy-done.2, s32[4,64,128]{2,1,0:T(8,128)S(1)} %copy-done.3), custom_call_target="tpu_custom_call" | custom-call | tf_op jit(solution)/shard_map/pallas_call | solution.py:454
  66.1 0.8 %copy.6 = f32[4,4,64,128]{3,2,1,0:T(8,128)} copy(f32[4,4,64,128]{3,2,1,0:T(8,128)S(1)} %shard_map.46) | data formatting | bytes 1048576
Async XLA Ops:
  0.0 1.0 %copy-start = (f32[4,4,64,128]{3,2,1,0:T(8,128)S(1)}, f32[4,4,64,128]{3,2,1,0:T(8,128)}, u32[]{:S(2)}) copy-start(f32[4,4,64,128]{3,2,1,0:T(8,128)} %fields.1) | copy-start | bytes 1572868
  1.0 0.9 %copy-start.1 = (s32[4,64,128]{2,1,0:T(8,128)S(1)}, s32[4,64,128]{2,1,0:T(8,128)}, u32[]{:S(2)}) copy-start(s32[4,64,128]{2,1,0:T(8,128)} %volume_code.1) | copy-start | bytes 393220
  1.9 0.9 %copy-start.2 = (s32[4,64,128]{2,1,0:T(8,128)S(1)}, s32[4,64,128]{2,1,0:T(8,128)}, u32[]{:S(2)}) copy-start(s32[4,64,128]{2,1,0:T(8,128)} %cut_flag.1) | copy-start | bytes 393220
  2.9 0.9 %copy-start.3 = (s32[4,64,128]{2,1,0:T(8,128)S(1)}, s32[4,64,128]{2,1,0:T(8,128)}, u32[]{:S(2)}) copy-start(s32[4,64,128]{2,1,0:T(8,128)} %member_bits.1) | copy-start | bytes 393220
where the time goes:
time: 67.1 us; the launch traced here: 66.9 us
  Pallas kernels  62.4 us (93%)
  local copies, waits for them, and re-layouts  4.55 us (7%)
    pallas_call x1, Pallas kernels, body(): pl.pallas_call(kernel, out_shape=jax.ShapeDtypeStruct((FIELDS,) + block,...  62.4 us
    unnamed x9, local copies, waits for them, and re-layouts  4.55 us

commit v1 on v0

v1 whole, which is shorter than its diff:
```python
import jax
import jax.numpy as jnp
from jax import lax
from jax.experimental import pallas as pl
from jax.experimental.pallas import tpu as pltpu
from jax.sharding import PartitionSpec as P

MESH = pl.DeviceIdType.MESH
FIELDS = 4
LAYERS = 4
ROWS = 64
TILES = ROWS // 8
PADDED = ROWS + 16
LANES = 128
CHUNK = 16
CHUNKS = ROWS // CHUNK
SIGNS = (-1, 1)

TRAVEL = []
for kind in ((1, 0, 0), (1, 1, 0), (1, 0, 1), (1, 1, 1), (0, 0, 1), (0, 1, 0), (0, 1, 1)):
    for sx in SIGNS if kind[0] else (0,):
        for sy in SIGNS if kind[1] else (0,):
            for sz in SIGNS if kind[2] else (0,):
                TRAVEL.append((sx, sy, sz))
MESSAGES = []
for travel in TRAVEL:
    for chunk in range(CHUNKS if travel[1:] == (0, 0) else 1):
        MESSAGES.append(travel + (chunk,))


def side(sign):
    return (sign + 1) // 2


def offset_bit(dx, dy, dz):
    return 9 * (dx + 1) + 3 * (dy + 1) + (dz + 1)


def neighbour(travel):
    result = {}
    for axis, sign in zip(("gx", "gy", "gz"), travel):
        if sign:
            count = lax.axis_size(axis)
            result[axis] = lax.rem(lax.axis_index(axis) + sign + count, count)
    return result


def turn(value, shift):
    if isinstance(shift, int):
        shift = shift % LANES
        if shift == 0:
            return value
    return pltpu.roll(value, shift, 1)


def kernel(fields, volume_code, cut_flag, member_bits, result, raw, code, cut, bits, act, kap, inv_count,
           inv_volume, w, acc, hats, xface, yrows, edges, zpack, xzpack, yzpack, cpack,
           rx, ry, re, rz, rxz, ryz, rc, in_sem, send_sem, recv_sem):
    lane8 = lax.broadcasted_iota(jnp.int32, (8, LANES), 1)
    lane1 = lax.broadcasted_iota(jnp.int32, (1, LANES), 1)
    zero8 = jnp.zeros((8, LANES), jnp.float32)

    loads = []
    for index, (source, target) in enumerate(
        ((volume_code, code), (cut_flag, cut), (member_bits, bits), (fields, raw))
    ):
        copy = pltpu.make_async_copy(source, target, in_sem.at[index])
        copy.start()
        loads.append(copy)
    barrier = pltpu.get_barrier_semaphore()
    for travel in TRAVEL:
        pl.semaphore_signal(barrier, inc=1, device_id=neighbour(travel), device_id_type=MESH)

    for x in range(LAYERS):
        for rows in (0, PADDED - 8):
            act[x, rows : rows + 8, :] = jnp.zeros((8, LANES), jnp.int32)
            for f in range(FIELDS + 1):
                w[f, x, rows : rows + 8, :] = zero8
    for copy in loads:
        copy.wait()

    def prepare(t, carry):
        own = pl.ds(pl.multiple_of(8 * t, 8), 8)
        padded = pl.ds(pl.multiple_of(8 * t + 8, 8), 8)
        for x in range(LAYERS):
            kappa = code[x, own, :].astype(jnp.float32) * (1.0 / 1048576.0)
            active = bits[x, own, :] * cut[x, own, :]
            act[x, padded, :] = active
            kap[x, own, :] = kappa
            others = lax.population_count(jnp.bitwise_and(active, ((1 << 27) - 1) ^ (1 << 13)))
            inv_count[x, own, :] = 1.0 / (others + 1).astype(jnp.float32)
            w[FIELDS, x, padded, :] = kappa
            for f in range(FIELDS):
                w[f, x, padded, :] = kappa * raw[f, x, own, :]
        return carry

    lax.fori_loop(0, TILES, prepare, 0)

    def message(stage, sx, sy, sz, chunk):
        count = FIELDS + 1 if stage == 0 else FIELDS
        which = stage // 2
        ix, iy, iz = side(sx), side(sy), side(sz)
        e = 2 * ix + iy
        if sx and not sy and not sz:
            start = chunk * CHUNK
            if stage % 2 == 0:
                source = xface.at[which, ix, 0:count, start : start + CHUNK, :]
                target = rx.at[which, ix, 0:count, start : start + CHUNK, :]
            else:
                mid = hats.at[which, 1]
                source = mid.at[:, 4 if sx == 1 else 1, 8 + start : 8 + start + CHUNK, :]
                target = mid.at[:, 0 if sx == 1 else 5, 8 + start : 8 + start + CHUNK, :]
        elif sy and not sx and not sz:
            source, target = yrows.at[stage, iy], ry.at[stage, iy]
        elif sz and not sx and not sy:
            source, target = zpack.at[stage], rz.at[stage, iz]
        elif sx and sy and not sz:
            source, target = edges.at[stage, e], re.at[stage, e]
        elif sx and sz and not sy:
            source, target = xzpack.at[stage, ix], rxz.at[stage, ix, iz]
        elif sy and sz and not sx:
            source, target = yzpack.at[stage, iy], ryz.at[stage, iy, iz]
        else:
            source, target = cpack.at[stage, e], rc.at[stage, e, iz]
        index = MESSAGES.index((sx, sy, sz, chunk))
        return pltpu.make_async_remote_copy(
            src_ref=source,
            dst_ref=target,
            send_sem=send_sem.at[stage, index],
            recv_sem=recv_sem.at[stage, index],
            device_id=neighbour((sx, sy, sz)),
            device_id_type=MESH,
        )

    def send(stage, chosen):
        for which in MESSAGES:
            if chosen(*which):
                message(stage, *which).start()

    def receive(stage, chosen):
        for which in MESSAGES:
            if chosen(*which):
                message(stage, *which).wait_recv()

    def drain(stage):
        for which in MESSAGES:
            message(stage, *which).wait_send()

    def beside(sx, sy, sz, chunk):
        return sx == 0

    def small(sx, sy, sz, chunk):
        return sx != 0 and (sy != 0 or sz != 0)

    def faces(wanted):
        return lambda sx, sy, sz, chunk: sx != 0 and sy == 0 and sz == 0 and chunk in wanted

    def packed(base, value, p, lane):
        return jnp.where(jnp.right_shift(lane, 1) == p, turn(value, 1 + 2 * p), base)

    def pairs(from_below, from_above, lane):
        return jnp.where(jnp.bitwise_and(lane, 1) == 1, turn(from_below, 1), turn(from_above, -1))

    def placed(pack, p):
        return turn(pack, LANES - 1 - 2 * p)

    def only_ends(value, lane):
        return jnp.where((lane == 0) | (lane == LANES - 1), value, 0.0)

    def pushed(xt, row, dys, count):
        sums = [[None] * count for _ in range(3)]
        for dx in (-1, 0, 1):
            xs = xt - dx
            if xs < 0 or xs >= LAYERS:
                continue
            for dy in dys:
                rows = pl.ds(row - dy, 8)
                active = act[xs, rows, :]
                values = [w[f, xs, rows, :] for f in range(count)]
                for dz in (-1, 0, 1):
                    bit = offset_bit(dx, dy, dz)
                    if bit != 13:
                        chosen = jnp.bitwise_and(active, 1 << bit) != 0
                    for f in range(count):
                        term = values[f] if bit == 13 else jnp.where(chosen, values[f], 0.0)
                        old = sums[dz + 1][f]
                        sums[dz + 1][f] = term if old is None else old + term
        mains, ends = [], []
        for f in range(count):
            up = turn(sums[2][f], 1)
            down = turn(sums[0][f], -1)
            mains.append(
                sums[1][f] + jnp.where(lane8 == 0, 0.0, up) + jnp.where(lane8 == LANES - 1, 0.0, down)
            )
            ends.append(jnp.where(lane8 < LANES // 2, sums[0][f], sums[2][f]))
        return mains, ends

    def scatter(stage, count):
        which = stage // 2
        for sx in SIGNS:
            xt = -1 if sx == -1 else LAYERS
            ix = side(sx)
            pack = zero8
            for t in range(TILES):
                mains, ends = pushed(xt, 8 * t + 8, (-1, 0, 1), count)
                for f in range(count):
                    xface[which, ix, f, 8 * t : 8 * t + 8, :] = mains[f]
                    pack = packed(pack, ends[f], count * t + f, lane8)
            xzpack[stage, ix] = pack
            for sy in SIGNS:
                mains, ends = pushed(xt, 0 if sy == -1 else PADDED - 8, (sy,), count)
                row = 7 if sy == -1 else 0
                e = 2 * ix + side(sy)
                pack = zero8
                for f in range(count):
                    edges[stage, e, f : f + 1, :] = mains[f][row : row + 1, :]
                    pack = packed(pack, ends[f], f, lane8)
                cpack[stage, e] = pack[row : row + 1, :]
        if stage == 0:
            pl.semaphore_wait(barrier, len(TRAVEL))
        send(stage, small)
        send(stage, faces(range(CHUNKS)))

        def rest(t, carry):
            own = pl.ds(pl.multiple_of(8 * t, 8), 8)
            pack = zero8
            for xt in range(LAYERS):
                mains, ends = pushed(xt, 8 * t + 8, (-1, 0, 1), count)
                for f in range(count):
                    acc[f, xt, own, :] = mains[f]
                    pack = packed(pack, ends[f], 4 * f + xt, lane8)
            zpack[stage, t] = pack
            return carry

        lax.fori_loop(0, TILES, rest, 0)
        send(stage, lambda sx, sy, sz, chunk: (sx, sy) == (0, 0))
        for sy in SIGNS:
            row = 7 if sy == -1 else 0
            pack = zero8
            for xt in range(LAYERS):
                mains, ends = pushed(xt, 0 if sy == -1 else PADDED - 8, (sy,), count)
                for f in range(count):
                    p = 4 * f + xt
                    yrows[stage, side(sy), p : p + 1, :] = mains[f][row : row + 1, :]
                    pack = packed(pack, ends[f], p, lane8)
            yzpack[stage, side(sy)] = pack[row : row + 1, :]
        send(stage, lambda sx, sy, sz, chunk: sx == 0 and sy != 0)

    def combine(stage, count):
        odd = stage + 1
        which = stage // 2

        def finish(x, t, sums):
            own = pl.ds(8 * t, 8)
            if stage == 0:
                inverse = 1.0 / sums[FIELDS]
                inv_volume[x, own, :] = inverse
            else:
                inverse = inv_volume[x, own, :]
            for f in range(FIELDS):
                hats[which, 1, f, x + 1, 8 * t + 8 : 8 * t + 16, :] = sums[f] * inverse

        receive(stage, beside)
        for sy in SIGNS:
            iy = side(sy)
            row = 0 if sy == 1 else ROWS - 1
            yz = pairs(ryz[stage, iy, 1], ryz[stage, iy, 0], lane1)
            for x in range(LAYERS):
                for f in range(count):
                    p = 4 * f + x
                    value = ry[stage, iy, p : p + 1, :] + only_ends(placed(yz, p), lane1)
                    acc[f, x, row : row + 1, :] += value
        for t in range(TILES):
            z = pairs(rz[stage, 1, t], rz[stage, 0, t], lane8)
            for x in range(LAYERS):
                sums = []
                for f in range(count):
                    value = acc[f, x, 8 * t : 8 * t + 8, :] + only_ends(placed(z, 4 * f + x), lane8)
                    sums.append(value)
                if x in (0, LAYERS - 1):
                    for f in range(count):
                        acc[f, x, 8 * t : 8 * t + 8, :] = sums[f]
                else:
                    finish(x, t, sums)
        receive(stage, small)
        for sx in SIGNS:
            ix = side(sx)
            x = 0 if sx == 1 else LAYERS - 1
            xz = pairs(rxz[stage, ix, 1], rxz[stage, ix, 0], lane8)
            for t in range(TILES):
                for f in range(count):
                    acc[f, x, 8 * t : 8 * t + 8, :] += only_ends(placed(xz, count * t + f), lane8)
            for sy in SIGNS:
                e = 2 * ix + side(sy)
                row = 0 if sy == 1 else ROWS - 1
                corner = pairs(rc[stage, e, 1], rc[stage, e, 0], lane1)
                for f in range(count):
                    value = re[stage, e, f : f + 1, :] + only_ends(placed(corner, f), lane1)
                    acc[f, x, row : row + 1, :] += value
        for chunk in range(CHUNKS):
            receive(stage, faces((chunk,)))
            for t in range(chunk * CHUNK // 8, (chunk + 1) * CHUNK // 8):
                for sx in SIGNS:
                    x = 0 if sx == 1 else LAYERS - 1
                    sums = []
                    for f in range(count):
                        own = slice(8 * t, 8 * t + 8)
                        sums.append(acc[f, x, own, :] + rx[which, side(sx), f, own, :])
                    finish(x, t, sums)
            send(odd, faces((chunk,)))
        for sx in SIGNS:
            x = 0 if sx == -1 else LAYERS - 1
            pack = zero8
            for t in range(TILES):
                for f in range(FIELDS):
                    value = hats[which, 1, f, x + 1, 8 * t + 8 : 8 * t + 16, :]
                    pack = packed(pack, value, FIELDS * t + f, lane8)
            xzpack[odd, side(sx)] = pack
            for sy in SIGNS:
                row = 8 if sy == -1 else 7 + ROWS
                e = 2 * side(sx) + side(sy)
                pack = jnp.zeros((1, LANES), jnp.float32)
                for f in range(FIELDS):
                    value = hats[which, 1, f, x + 1, row : row + 1, :]
                    edges[odd, e, f : f + 1, :] = value
                    pack = packed(pack, value, f, lane1)
                cpack[odd, e] = pack
        send(odd, small)
        for t in range(TILES):
            pack = zero8
            for x in range(LAYERS):
                for f in range(FIELDS):
                    value = hats[which, 1, f, x + 1, 8 * t + 8 : 8 * t + 16, :]
                    pack = packed(pack, value, 4 * f + x, lane8)
            zpack[odd, t] = pack
        send(odd, lambda sx, sy, sz, chunk: (sx, sy) == (0, 0))
        for sy in SIGNS:
            row = 8 if sy == -1 else 7 + ROWS
            for x in range(LAYERS):
                for f in range(FIELDS):
                    p = 4 * f + x
                    yrows[odd, side(sy), p : p + 1, :] = hats[which, 1, f, x + 1, row : row + 1, :]
            t = 0 if sy == -1 else TILES - 1
            yzpack[odd, side(sy)] = zpack[odd, t, row % 8 : row % 8 + 1, :]
        send(odd, lambda sx, sy, sz, chunk: sx == 0 and sy != 0)
        drain(stage)

    def gather(stage, last):
        which = stage // 2

        def shifted(f, xi, rows, value, ends, lane):
            hats[which, 2, f, xi, rows, :] = jnp.where(lane == LANES - 1, ends, turn(value, -1))
            hats[which, 0, f, xi, rows, :] = jnp.where(lane == 0, ends, turn(value, 1))

        def pulled(sums, x, t, dxs):
            active = act[x, pl.ds(pl.multiple_of(8 * t + 8, 8), 8), :]
            for dx in dxs:
                if sums is None:
                    sums = [hats[which, 1, f, x + 1, pl.ds(8 * t + 8, 8), :] for f in range(FIELDS)]
                for dy in (-1, 0, 1):
                    for dz in (-1, 0, 1):
                        bit = offset_bit(dx, dy, dz)
                        if bit == 13:
                            continue
                        chosen = jnp.bitwise_and(active, 1 << bit) != 0
                        rows = pl.ds(8 * t + 8 + dy, 8)
                        for f in range(FIELDS):
                            value = hats[which, dz + 1, f, x + 1 + dx, rows, :]
                            sums[f] = sums[f] + jnp.where(chosen, value, 0.0)
            return sums

        def finish(x, t, sums):
            own = pl.ds(pl.multiple_of(8 * t, 8), 8)
            scale = inv_count[x, own, :]
            if not last:
                scale = scale * kap[x, own, :]
            for f in range(FIELDS):
                if last:
                    result[f, x, own, :] = sums[f] * scale
                else:
                    w[f, x, pl.ds(pl.multiple_of(8 * t + 8, 8), 8), :] = sums[f] * scale

        receive(stage, beside)
        for sy in SIGNS:
            iy = side(sy)
            row = 7 if sy == 1 else 8 + ROWS
            yz = pairs(ryz[stage, iy, 1], ryz[stage, iy, 0], lane1)
            for x in range(LAYERS):
                for f in range(FIELDS):
                    p = 4 * f + x
                    value = ry[stage, iy, p : p + 1, :]
                    hats[which, 1, f, x + 1, row : row + 1, :] = value
                    shifted(f, x + 1, slice(row, row + 1), value, placed(yz, p), lane1)

        def shifts(t, carry):
            z = pairs(rz[stage, 1, t], rz[stage, 0, t], lane8)
            padded = pl.ds(pl.multiple_of(8 * t + 8, 8), 8)
            for x in range(LAYERS):
                for f in range(FIELDS):
                    value = hats[which, 1, f, x + 1, padded, :]
                    shifted(f, x + 1, padded, value, placed(z, 4 * f + x), lane8)
            return carry

        lax.fori_loop(0, TILES, shifts, 0)

        def interior(t, carry):
            for x in range(LAYERS):
                if x == 0:
                    sums = pulled(None, x, t, (0, 1))
                elif x == LAYERS - 1:
                    sums = pulled(None, x, t, (-1, 0))
                else:
                    finish(x, t, pulled(None, x, t, (-1, 0, 1)))
                    continue
                for f in range(FIELDS):
                    acc[f, x, pl.ds(pl.multiple_of(8 * t, 8), 8), :] = sums[f]
            return carry

        lax.fori_loop(0, TILES, interior, 0)
        receive(stage, lambda sx, sy, sz, chunk: sx != 0)
        for sx in SIGNS:
            ix = side(sx)
            xi = 0 if sx == 1 else LAYERS + 1
            for sy in SIGNS:
                e = 2 * ix + side(sy)
                row = 7 if sy == 1 else 8 + ROWS
                corner = pairs(rc[stage, e, 1], rc[stage, e, 0], lane1)
                for f in range(FIELDS):
                    value = re[stage, e, f : f + 1, :]
                    hats[which, 1, f, xi, row : row + 1, :] = value
                    shifted(f, xi, slice(row, row + 1), value, placed(corner, f), lane1)
            xz = pairs(rxz[stage, ix, 1], rxz[stage, ix, 0], lane8)
            for t in range(TILES):
                rows = slice(8 * t + 8, 8 * t + 16)
                for f in range(FIELDS):
                    shifted(f, xi, rows, hats[which, 1, f, xi, rows, :], placed(xz, FIELDS * t + f), lane8)

        def boundary(t, carry):
            for x, dx in ((0, -1), (LAYERS - 1, 1)):
                sums = [acc[f, x, pl.ds(pl.multiple_of(8 * t, 8), 8), :] for f in range(FIELDS)]
                finish(x, t, pulled(sums, x, t, (dx,)))
            return carry

        lax.fori_loop(0, TILES, boundary, 0, unroll=4)

    scatter(0, FIELDS + 1)
    combine(0, FIELDS + 1)
    gather(1, False)
    scatter(2, FIELDS)
    drain(1)
    combine(2, FIELDS)
    gather(3, True)
    drain(3)


def body(fields, volume_code, cut_flag, member_bits):
    f32, i32 = jnp.float32, jnp.int32
    vmem = pltpu.VMEM
    block = (LAYERS, ROWS, LANES)
    padded = (LAYERS, PADDED, LANES)
    row_count = 24
    scratch = [
        vmem((FIELDS,) + block, f32),
        vmem(block, i32),
        vmem(block, i32),
        vmem(block, i32),
        vmem(padded, i32),
        vmem(block, f32),
        vmem(block, f32),
        vmem(block, f32),
        vmem((FIELDS + 1,) + padded, f32),
        vmem((FIELDS + 1,) + block, f32),
        vmem((2, 3, FIELDS, LAYERS + 2, PADDED, LANES), f32),
        vmem((2, 2, FIELDS + 1, ROWS, LANES), f32),
        vmem((4, 2, row_count, LANES), f32),
        vmem((4, 4, 8, LANES), f32),
        vmem((4, TILES, 8, LANES), f32),
        vmem((4, 2, 8, LANES), f32),
        vmem((4, 2, 1, LANES), f32),
        vmem((4, 4, 1, LANES), f32),
        vmem((2, 2, FIELDS + 1, ROWS, LANES), f32),
        vmem((4, 2, row_count, LANES), f32),
        vmem((4, 4, 8, LANES), f32),
        vmem((4, 2, TILES, 8, LANES), f32),
        vmem((4, 2, 2, 8, LANES), f32),
        vmem((4, 2, 2, 1, LANES), f32),
        vmem((4, 4, 2, 1, LANES), f32),
        pltpu.SemaphoreType.DMA((4,)),
        pltpu.SemaphoreType.DMA((4, len(MESSAGES))),
        pltpu.SemaphoreType.DMA((4, len(MESSAGES))),
    ]
    in_hbm = pl.BlockSpec(memory_space=pltpu.MemorySpace.HBM)
    in_vmem = pl.BlockSpec(memory_space=pltpu.MemorySpace.VMEM)
    return pl.pallas_call(
        kernel,
        out_shape=jax.ShapeDtypeStruct((FIELDS,) + block, f32),
        in_specs=[in_hbm] * 4,
        out_specs=in_vmem,
        scratch_shapes=scratch,
        compiler_params=pltpu.CompilerParams(
            collective_id=0, has_side_effects=True, vmem_limit_bytes=67043328
        ),
    )(fields, volume_code, cut_flag, member_bits)


def solution(mesh):
    in_specs = (
        P(None, "gx", "gy", "gz"),
        P("gx", "gy", "gz"),
        P("gx", "gy", "gz"),
        P("gx", "gy", "gz"),
    )
    out_specs = P(None, "gx", "gy", "gz")
    return jax.shard_map(body, mesh=mesh, in_specs=in_specs, out_specs=out_specs, check_vma=False)
```

time: 67.1 us -> 50.6 us (0.75)
  Pallas kernels: 62.4 us -> 48.6 us
  local copies, waits for them, and re-layouts: 4.55 us -> 1.89 us
    pallas_call x1, Pallas kernels: 62.4 us -> 48.6 us  [body(): pl.pallas_call(kernel, out_shape=jax.ShapeDtypeStruct((FIELDS,) + block,...]
    unnamed x9 -> x1, local copies, waits for them, and re-layouts: 4.55 us -> 1.89 us
where the time goes in v1:
time: 50.6 us; the launch traced here: 50.5 us
  Pallas kernels  48.6 us (96%)
  local copies, waits for them, and re-layouts  1.89 us (4%)
    pallas_call x1, Pallas kernels, body(): pl.pallas_call(kernel, out_shape=jax.ShapeDtypeStruct((FIELDS,) + block,...  48.6 us
    unnamed x1, local copies, waits for them, and re-layouts  1.89 us

profile of v1, /device:TPU:1, one launch (start us, length us, event | category | flops | bytes accessed | tf_op | source)
XLA Modules:
  0.0 50.5 jit_solution(2086528825635678763)
XLA Ops:
  0.0 48.6 %shard_map.46 = f32[4,4,64,128]{3,2,1,0:T(8,128)} custom-call(f32[4,4,64,128]{3,2,1,0:T(8,128)} %fields.1, s32[4,64,128]{2,1,0:T(8,128)} %volume_code.1, s32[4,64,128]{2,1,0:T(8,128)} %cut_flag.1, s32[4,64,128]{2,1,0:T(8,128)} %member_bits.1), custom_call_target="tpu_custom_call" | custom-call | tf_op jit(solution)/shard_map/pallas_call | solution.py:494
  48.6 1.9 %copy.6 = f32[4,4,64,128]{3,2,1,0:T(8,128)} copy(f32[4,4,64,128]{3,2,1,0:T(8,128)} %shard_map.46) | data formatting | bytes 1048576

commit v2 on v1

--- a/solution.py
+++ b/solution.py
@@ -14,6 +14,8 @@
 LANES = 128
 CHUNK = 16
 CHUNKS = ROWS // CHUNK
+ORDER = (0, CHUNKS - 1) + tuple(range(1, CHUNKS - 1))
+ROW_COUNT = 24
 SIGNS = (-1, 1)
 
 TRAVEL = []
@@ -55,7 +57,7 @@
 
 def kernel(fields, volume_code, cut_flag, member_bits, result, raw, code, cut, bits, act, kap, inv_count,
            inv_volume, w, acc, hats, xface, yrows, edges, zpack, xzpack, yzpack, cpack,
-           rx, ry, re, rz, rxz, ryz, rc, in_sem, send_sem, recv_sem):
+           rx, ry, re, rz, rxz, ryz, rc, in_sem, send_sem, recv_sem, lengths):
     lane8 = lax.broadcasted_iota(jnp.int32, (8, LANES), 1)
     lane1 = lax.broadcasted_iota(jnp.int32, (1, LANES), 1)
     zero8 = jnp.zeros((8, LANES), jnp.float32)
@@ -122,12 +124,12 @@
             source, target = yzpack.at[stage, iy], ryz.at[stage, iy, iz]
         else:
             source, target = cpack.at[stage, e], rc.at[stage, e, iz]
-        index = MESSAGES.index((sx, sy, sz, chunk))
+        group = 0 if sx == 0 else 1 if sy or sz else 2 + chunk
         return pltpu.make_async_remote_copy(
             src_ref=source,
             dst_ref=target,
-            send_sem=send_sem.at[stage, index],
-            recv_sem=recv_sem.at[stage, index],
+            send_sem=send_sem.at[stage],
+            recv_sem=recv_sem.at[stage, group],
             device_id=neighbour((sx, sy, sz)),
             device_id_type=MESH,
         )
@@ -137,14 +139,27 @@
             if chosen(*which):
                 message(stage, *which).start()
 
-    def receive(stage, chosen):
-        for which in MESSAGES:
-            if chosen(*which):
-                message(stage, *which).wait_recv()
+    def rows_of(stage, which):
+        sx, sy, sz, chunk = which
+        if (sy, sz) == (0, 0):
+            return CHUNK * (FIELDS + 1 if stage == 0 else FIELDS)
+        if (sx, sz) == (0, 0):
+            return ROW_COUNT
+        if (sx, sy) == (0, 0):
+            return ROWS
+        return 8 if sx and not (sy and sz) else 1
+
+    def await_rows(semaphore, rows):
+        part = lengths.at[0:rows]
+        pltpu.make_async_copy(part, part, semaphore).wait()
+
+    def receive(stage, group):
+        chosen = [beside, small, None][min(group, 2)] or faces((group - 2,))
+        rows = sum(rows_of(stage, which) for which in MESSAGES if chosen(*which))
+        await_rows(recv_sem.at[stage, group], rows)
 
     def drain(stage):
-        for which in MESSAGES:
-            message(stage, *which).wait_send()
+        await_rows(send_sem.at[stage], sum(rows_of(stage, which) for which in MESSAGES))
 
     def beside(sx, sy, sz, chunk):
         return sx == 0
@@ -200,13 +215,6 @@
         for sx in SIGNS:
             xt = -1 if sx == -1 else LAYERS
             ix = side(sx)
-            pack = zero8
-            for t in range(TILES):
-                mains, ends = pushed(xt, 8 * t + 8, (-1, 0, 1), count)
-                for f in range(count):
-                    xface[which, ix, f, 8 * t : 8 * t + 8, :] = mains[f]
-                    pack = packed(pack, ends[f], count * t + f, lane8)
-            xzpack[stage, ix] = pack
             for sy in SIGNS:
                 mains, ends = pushed(xt, 0 if sy == -1 else PADDED - 8, (sy,), count)
                 row = 7 if sy == -1 else 0
@@ -218,8 +226,20 @@
                 cpack[stage, e] = pack[row : row + 1, :]
         if stage == 0:
             pl.semaphore_wait(barrier, len(TRAVEL))
-        send(stage, small)
-        send(stage, faces(range(CHUNKS)))
+        send(stage, lambda sx, sy, sz, chunk: sx != 0 and sy != 0)
+        for sx in SIGNS:
+            xt = -1 if sx == -1 else LAYERS
+            ix = side(sx)
+            pack = zero8
+            for t in range(TILES):
+                mains, ends = pushed(xt, 8 * t + 8, (-1, 0, 1), count)
+                for f in range(count):
+                    xface[which, ix, f, 8 * t : 8 * t + 8, :] = mains[f]
+                    pack = packed(pack, ends[f], count * t + f, lane8)
+            xzpack[stage, ix] = pack
+        send(stage, lambda sx, sy, sz, chunk: sx != 0 and sy == 0 and sz != 0)
+        for chunk in ORDER:
+            send(stage, faces((chunk,)))
 
         def rest(t, carry):
             own = pl.ds(pl.multiple_of(8 * t, 8), 8)
@@ -260,7 +280,7 @@
             for f in range(FIELDS):
                 hats[which, 1, f, x + 1, 8 * t + 8 : 8 * t + 16, :] = sums[f] * inverse
 
-        receive(stage, beside)
+        receive(stage, 0)
         for sy in SIGNS:
             iy = side(sy)
             row = 0 if sy == 1 else ROWS - 1
@@ -282,7 +302,7 @@
                         acc[f, x, 8 * t : 8 * t + 8, :] = sums[f]
                 else:
                     finish(x, t, sums)
-        receive(stage, small)
+        receive(stage, 1)
         for sx in SIGNS:
             ix = side(sx)
             x = 0 if sx == 1 else LAYERS - 1
@@ -297,8 +317,8 @@
                 for f in range(count):
                     value = re[stage, e, f : f + 1, :] + only_ends(placed(corner, f), lane1)
                     acc[f, x, row : row + 1, :] += value
-        for chunk in range(CHUNKS):
-            receive(stage, faces((chunk,)))
+        for position, chunk in enumerate(ORDER):
+            receive(stage, 2 + chunk)
             for t in range(chunk * CHUNK // 8, (chunk + 1) * CHUNK // 8):
                 for sx in SIGNS:
                     x = 0 if sx == 1 else LAYERS - 1
@@ -307,25 +327,30 @@
                         own = slice(8 * t, 8 * t + 8)
                         sums.append(acc[f, x, own, :] + rx[which, side(sx), f, own, :])
                     finish(x, t, sums)
+            if position == 1:
+                for sx in SIGNS:
+                    x = 0 if sx == -1 else LAYERS - 1
+                    for sy in SIGNS:
+                        row = 8 if sy == -1 else 7 + ROWS
+                        e = 2 * side(sx) + side(sy)
+                        pack = jnp.zeros((1, LANES), jnp.float32)
+                        for f in range(FIELDS):
+                            value = hats[which, 1, f, x + 1, row : row + 1, :]
+                            edges[odd, e, f : f + 1, :] = value
+                            pack = packed(pack, value, f, lane1)
+                        cpack[odd, e] = pack
+                send(odd, lambda sx, sy, sz, chunk: sx != 0 and sy != 0)
+            if position == CHUNKS - 1:
+                for sx in SIGNS:
+                    x = 0 if sx == -1 else LAYERS - 1
+                    pack = zero8
+                    for t in range(TILES):
+                        for f in range(FIELDS):
+                            value = hats[which, 1, f, x + 1, 8 * t + 8 : 8 * t + 16, :]
+                            pack = packed(pack, value, FIELDS * t + f, lane8)
+                    xzpack[odd, side(sx)] = pack
+                send(odd, lambda sx, sy, sz, chunk: sx != 0 and sy == 0 and sz != 0)
             send(odd, faces((chunk,)))
-        for sx in SIGNS:
-            x = 0 if sx == -1 else LAYERS - 1
-            pack = zero8
-            for t in range(TILES):
-                for f in range(FIELDS):
-                    value = hats[which, 1, f, x + 1, 8 * t + 8 : 8 * t + 16, :]
-                    pack = packed(pack, value, FIELDS * t + f, lane8)
-            xzpack[odd, side(sx)] = pack
-            for sy in SIGNS:
-                row = 8 if sy == -1 else 7 + ROWS
-                e = 2 * side(sx) + side(sy)
-                pack = jnp.zeros((1, LANES), jnp.float32)
-                for f in range(FIELDS):
-                    value = hats[which, 1, f, x + 1, row : row + 1, :]
-                    edges[odd, e, f : f + 1, :] = value
-                    pack = packed(pack, value, f, lane1)
-                cpack[odd, e] = pack
-        send(odd, small)
         for t in range(TILES):
             pack = zero8
             for x in range(LAYERS):
@@ -380,7 +405,17 @@
                 else:
                     w[f, x, pl.ds(pl.multiple_of(8 * t + 8, 8), 8), :] = sums[f] * scale
 
-        receive(stage, beside)
+        def rotations(t, carry):
+            padded = pl.ds(pl.multiple_of(8 * t + 8, 8), 8)
+            for x in range(LAYERS):
+                for f in range(FIELDS):
+                    value = hats[which, 1, f, x + 1, padded, :]
+                    hats[which, 2, f, x + 1, padded, :] = turn(value, -1)
+                    hats[which, 0, f, x + 1, padded, :] = turn(value, 1)
+            return carry
+
+        lax.fori_loop(0, TILES, rotations, 0)
+        receive(stage, 0)
         for sy in SIGNS:
             iy = side(sy)
             row = 7 if sy == 1 else 8 + ROWS
@@ -392,16 +427,18 @@
                     hats[which, 1, f, x + 1, row : row + 1, :] = value
                     shifted(f, x + 1, slice(row, row + 1), value, placed(yz, p), lane1)
 
-        def shifts(t, carry):
+        def new_ends(t, carry):
             z = pairs(rz[stage, 1, t], rz[stage, 0, t], lane8)
             padded = pl.ds(pl.multiple_of(8 * t + 8, 8), 8)
             for x in range(LAYERS):
                 for f in range(FIELDS):
-                    value = hats[which, 1, f, x + 1, padded, :]
-                    shifted(f, x + 1, padded, value, placed(z, 4 * f + x), lane8)
+                    ends = placed(z, 4 * f + x)
+                    for k, lane in ((2, LANES - 1), (0, 0)):
+                        old = hats[which, k, f, x + 1, padded, :]
+                        hats[which, k, f, x + 1, padded, :] = jnp.where(lane8 == lane, ends, old)
             return carry
 
-        lax.fori_loop(0, TILES, shifts, 0)
+        lax.fori_loop(0, TILES, new_ends, 0)
 
         def interior(t, carry):
             for x in range(LAYERS):
@@ -417,7 +454,9 @@
             return carry
 
         lax.fori_loop(0, TILES, interior, 0)
-        receive(stage, lambda sx, sy, sz, chunk: sx != 0)
+        drain(stage)
+        for group in range(1, 2 + CHUNKS):
+            receive(stage, group)
         for sx in SIGNS:
             ix = side(sx)
             xi = 0 if sx == 1 else LAYERS + 1
@@ -447,10 +486,8 @@
     combine(0, FIELDS + 1)
     gather(1, False)
     scatter(2, FIELDS)
-    drain(1)
     combine(2, FIELDS)
     gather(3, True)
-    drain(3)
 
 
 def body(fields, volume_code, cut_flag, member_bits):
@@ -458,7 +495,6 @@
     vmem = pltpu.VMEM
     block = (LAYERS, ROWS, LANES)
     padded = (LAYERS, PADDED, LANES)
-    row_count = 24
     scratch = [
         vmem((FIELDS,) + block, f32),
         vmem(block, i32),
@@ -472,25 +508,27 @@
         vmem((FIELDS + 1,) + block, f32),
         vmem((2, 3, FIELDS, LAYERS + 2, PADDED, LANES), f32),
         vmem((2, 2, FIELDS + 1, ROWS, LANES), f32),
-        vmem((4, 2, row_count, LANES), f32),
+        vmem((4, 2, ROW_COUNT, LANES), f32),
         vmem((4, 4, 8, LANES), f32),
         vmem((4, TILES, 8, LANES), f32),
         vmem((4, 2, 8, LANES), f32),
         vmem((4, 2, 1, LANES), f32),
         vmem((4, 4, 1, LANES), f32),
         vmem((2, 2, FIELDS + 1, ROWS, LANES), f32),
-        vmem((4, 2, row_count, LANES), f32),
+        vmem((4, 2, ROW_COUNT, LANES), f32),
         vmem((4, 4, 8, LANES), f32),
         vmem((4, 2, TILES, 8, LANES), f32),
         vmem((4, 2, 2, 8, LANES), f32),
         vmem((4, 2, 2, 1, LANES), f32),
         vmem((4, 4, 2, 1, LANES), f32),
         pltpu.SemaphoreType.DMA((4,)),
-        pltpu.SemaphoreType.DMA((4, len(MESSAGES))),
-        pltpu.SemaphoreType.DMA((4, len(MESSAGES))),
+        pltpu.SemaphoreType.DMA((4,)),
+        pltpu.SemaphoreType.DMA((4, 2 + CHUNKS)),
+        vmem((1024, 1, LANES), f32),
     ]
     in_hbm = pl.BlockSpec(memory_space=pltpu.MemorySpace.HBM)
     in_vmem = pl.BlockSpec(memory_space=pltpu.MemorySpace.VMEM)
+    operands = (fields, volume_code, cut_flag, member_bits)
     return pl.pallas_call(
         kernel,
         out_shape=jax.ShapeDtypeStruct((FIELDS,) + block, f32),
@@ -498,9 +536,9 @@
         out_specs=in_vmem,
         scratch_shapes=scratch,
         compiler_params=pltpu.CompilerParams(
-            collective_id=0, has_side_effects=True, vmem_limit_bytes=67043328
+            collective_id=0, has_side_effects=True, vmem_limit_bytes=52000000
         ),
-    )(fields, volume_code, cut_flag, member_bits)
+    )(*[pltpu.with_memory_space_constraint(a, pltpu.MemorySpace.HBM) for a in operands])
 
 
 def solution(mesh):

time: 50.6 us -> 46.8 us (0.925)
  Pallas kernels: 48.6 us -> 45.9 us
  local copies, waits for them, and re-layouts: 1.89 us -> 0.8 us
    pallas_call x1, Pallas kernels: 48.6 us -> 45.9 us  [body(): pl.pallas_call(kernel, out_shape=jax.ShapeDtypeStruct((FIELDS,) + block,...]
    unnamed x1, local copies, waits for them, and re-layouts: 1.89 us -> 0.8 us
where the time goes in v2:
time: 46.8 us; the launch traced here: 46.7 us
  Pallas kernels  45.9 us (98%)
  local copies, waits for them, and re-layouts  0.8 us (2%)
    pallas_call x1, Pallas kernels, body(): pl.pallas_call(kernel, out_shape=jax.ShapeDtypeStruct((FIELDS,) + block,...  45.9 us

profile of v2, /device:TPU:1, one launch (start us, length us, event | category | flops | bytes accessed | tf_op | source)
XLA Modules:
  0.0 46.7 jit_solution(3362383295355706119)
XLA Ops:
  0.0 45.9 %shard_map.46 = f32[4,4,64,128]{3,2,1,0:T(8,128)S(1)} custom-call(f32[4,4,64,128]{3,2,1,0:T(8,128)} %fields.1, s32[4,64,128]{2,1,0:T(8,128)} %volume_code.1, s32[4,64,128]{2,1,0:T(8,128)} %cut_flag.1, s32[4,64,128]{2,1,0:T(8,128)} %member_bits.1), custom_call_target="tpu_custom_call" | custom-call | tf_op jit(solution)/shard_map/pallas_call | solution.py:532
  45.9 0.8 %copy.6 = f32[4,4,64,128]{3,2,1,0:T(8,128)} copy(f32[4,4,64,128]{3,2,1,0:T(8,128)S(1)} %shard_map.46) | data formatting | bytes 1048576

commit v3 on v2

--- a/solution.py
+++ b/solution.py
@@ -47,6 +47,16 @@
     return result
 
 
+def bits_of(dx=None, dy=None, dz=None):
+    result = 0
+    for x in (-1, 0, 1):
+        for y in (-1, 0, 1):
+            for z in (-1, 0, 1):
+                if dx in (None, x) and dy in (None, y) and dz in (None, z):
+                    result |= 1 << offset_bit(x, y, z)
+    return result
+
+
 def turn(value, shift):
     if isinstance(shift, int):
         shift = shift % LANES
@@ -57,7 +67,7 @@
 
 def kernel(fields, volume_code, cut_flag, member_bits, result, raw, code, cut, bits, act, kap, inv_count,
            inv_volume, w, acc, hats, xface, yrows, edges, zpack, xzpack, yzpack, cpack,
-           rx, ry, re, rz, rxz, ryz, rc, in_sem, send_sem, recv_sem, lengths):
+           rx, ry, re, rz, rxz, ryz, rc, in_sem, send_sem, recv_sem, lengths, inner, ends_act, beyond):
     lane8 = lax.broadcasted_iota(jnp.int32, (8, LANES), 1)
     lane1 = lax.broadcasted_iota(jnp.int32, (1, LANES), 1)
     zero8 = jnp.zeros((8, LANES), jnp.float32)
@@ -76,6 +86,7 @@
     for x in range(LAYERS):
         for rows in (0, PADDED - 8):
             act[x, rows : rows + 8, :] = jnp.zeros((8, LANES), jnp.int32)
+            beyond[rows : rows + 8, :] = zero8
             for f in range(FIELDS + 1):
                 w[f, x, rows : rows + 8, :] = zero8
     for copy in loads:
@@ -146,7 +157,7 @@
         if (sx, sz) == (0, 0):
             return ROW_COUNT
         if (sx, sy) == (0, 0):
-            return ROWS
+            return ROWS // 2
         return 8 if sx and not (sy and sz) else 1
 
     def await_rows(semaphore, rows):
@@ -209,6 +220,27 @@
             )
             ends.append(jnp.where(lane8 < LANES // 2, sums[0][f], sums[2][f]))
         return mains, ends
+
+    def split_bits(t, carry):
+        padded = pl.ds(pl.multiple_of(8 * t + 8, 8), 8)
+        own = pl.ds(pl.multiple_of(8 * t, 8), 8)
+        y = lax.broadcasted_iota(jnp.int32, (8, LANES), 0) + 8 * t
+        beyond_z = jnp.where(lane8 == 0, bits_of(dz=-1), 0) | jnp.where(lane8 == LANES - 1, bits_of(dz=1), 0)
+        beyond_y = jnp.where(y == 0, bits_of(dy=-1), 0) | jnp.where(y == ROWS - 1, bits_of(dy=1), 0)
+        columns = jnp.zeros((8, LANES), jnp.int32)
+        for x in range(LAYERS):
+            active = act[x, padded, :]
+            inner[x, own, :] = jnp.bitwise_and(active, jnp.bitwise_not(beyond_z | beyond_y))
+            columns = packed(columns, active, x, lane8)
+        columns = jnp.where(jnp.bitwise_and(lane8, 1) == 0, jnp.right_shift(columns, 2), columns)
+        x = jnp.bitwise_and(jnp.right_shift(lane8, 1), LAYERS - 1)
+        width = 2 * LAYERS
+        wide = jnp.where(lane8 < width, columns, 0)
+        for f in range(1, FIELDS):
+            wide = jnp.where(jnp.right_shift(lane8, 3) == f, turn(columns, width * f), wide)
+        beyond_x = jnp.where(x == 0, bits_of(dx=-1), 0) | jnp.where(x == LAYERS - 1, bits_of(dx=1), 0)
+        ends_act[t] = jnp.bitwise_and(wide, jnp.bitwise_not(beyond_x | beyond_y))
+        return carry
 
     def scatter(stage, count):
         which = stage // 2
@@ -241,19 +273,6 @@
         for chunk in ORDER:
             send(stage, faces((chunk,)))
 
-        def rest(t, carry):
-            own = pl.ds(pl.multiple_of(8 * t, 8), 8)
-            pack = zero8
-            for xt in range(LAYERS):
-                mains, ends = pushed(xt, 8 * t + 8, (-1, 0, 1), count)
-                for f in range(count):
-                    acc[f, xt, own, :] = mains[f]
-                    pack = packed(pack, ends[f], 4 * f + xt, lane8)
-            zpack[stage, t] = pack
-            return carry
-
-        lax.fori_loop(0, TILES, rest, 0)
-        send(stage, lambda sx, sy, sz, chunk: (sx, sy) == (0, 0))
         for sy in SIGNS:
             row = 7 if sy == -1 else 0
             pack = zero8
@@ -265,6 +284,24 @@
                     pack = packed(pack, ends[f], p, lane8)
             yzpack[stage, side(sy)] = pack[row : row + 1, :]
         send(stage, lambda sx, sy, sz, chunk: sx == 0 and sy != 0)
+        if stage == 0:
+            lax.fori_loop(0, TILES, split_bits, 0)
+
+        def rest(pair, carry):
+            pack = zero8
+            for half in range(2):
+                t = 2 * pair + half
+                own = pl.ds(pl.multiple_of(8 * t, 8), 8)
+                for xt in range(LAYERS):
+                    mains, ends = pushed(xt, 8 * t + 8, (-1, 0, 1), count)
+                    for f in range(count):
+                        acc[f, xt, own, :] = mains[f]
+                        pack = packed(pack, ends[f], 4 * f + xt + 32 * half, lane8)
+            zpack[stage, pair] = pack
+            return carry
+
+        lax.fori_loop(0, TILES // 2, rest, 0)
+        send(stage, lambda sx, sy, sz, chunk: (sx, sy) == (0, 0))
 
     def combine(stage, count):
         odd = stage + 1
@@ -291,11 +328,12 @@
                     value = ry[stage, iy, p : p + 1, :] + only_ends(placed(yz, p), lane1)
                     acc[f, x, row : row + 1, :] += value
         for t in range(TILES):
-            z = pairs(rz[stage, 1, t], rz[stage, 0, t], lane8)
+            if t % 2 == 0:
+                z = pairs(rz[stage, 1, t // 2], rz[stage, 0, t // 2], lane8)
             for x in range(LAYERS):
                 sums = []
                 for f in range(count):
-                    value = acc[f, x, 8 * t : 8 * t + 8, :] + only_ends(placed(z, 4 * f + x), lane8)
+                    value = acc[f, x, 8 * t : 8 * t + 8, :] + only_ends(placed(z, 4 * f + x + 32 * (t % 2)), lane8)
                     sums.append(value)
                 if x in (0, LAYERS - 1):
                     for f in range(count):
@@ -340,6 +378,17 @@
                             pack = packed(pack, value, f, lane1)
                         cpack[odd, e] = pack
                 send(odd, lambda sx, sy, sz, chunk: sx != 0 and sy != 0)
+                for sy in SIGNS:
+                    row = 8 if sy == -1 else 7 + ROWS
+                    pack = jnp.zeros((1, LANES), jnp.float32)
+                    for x in range(LAYERS):
+                        for f in range(FIELDS):
+                            p = 4 * f + x
+                            value = hats[which, 1, f, x + 1, row : row + 1, :]
+                            yrows[odd, side(sy), p : p + 1, :] = value
+                            pack = packed(pack, value, p, lane1)
+                    yzpack[odd, side(sy)] = pack
+                send(odd, lambda sx, sy, sz, chunk: sx == 0 and sy != 0)
             if position == CHUNKS - 1:
                 for sx in SIGNS:
                     x = 0 if sx == -1 else LAYERS - 1
@@ -351,23 +400,15 @@
                     xzpack[odd, side(sx)] = pack
                 send(odd, lambda sx, sy, sz, chunk: sx != 0 and sy == 0 and sz != 0)
             send(odd, faces((chunk,)))
-        for t in range(TILES):
+        for pair in range(TILES // 2):
             pack = zero8
-            for x in range(LAYERS):
-                for f in range(FIELDS):
-                    value = hats[which, 1, f, x + 1, 8 * t + 8 : 8 * t + 16, :]
-                    pack = packed(pack, value, 4 * f + x, lane8)
-            zpack[odd, t] = pack
+            for t in (2 * pair, 2 * pair + 1):
+                for x in range(LAYERS):
+                    for f in range(FIELDS):
+                        value = hats[which, 1, f, x + 1, 8 * t + 8 : 8 * t + 16, :]
+                        pack = packed(pack, value, 4 * f + x + 32 * (t % 2), lane8)
+            zpack[odd, pair] = pack
         send(odd, lambda sx, sy, sz, chunk: (sx, sy) == (0, 0))
-        for sy in SIGNS:
-            row = 8 if sy == -1 else 7 + ROWS
-            for x in range(LAYERS):
-                for f in range(FIELDS):
-                    p = 4 * f + x
-                    yrows[odd, side(sy), p : p + 1, :] = hats[which, 1, f, x + 1, row : row + 1, :]
-            t = 0 if sy == -1 else TILES - 1
-            yzpack[odd, side(sy)] = zpack[odd, t, row % 8 : row % 8 + 1, :]
-        send(odd, lambda sx, sy, sz, chunk: sx == 0 and sy != 0)
         drain(stage)
 
     def gather(stage, last):
@@ -377,8 +418,7 @@
             hats[which, 2, f, xi, rows, :] = jnp.where(lane == LANES - 1, ends, turn(value, -1))
             hats[which, 0, f, xi, rows, :] = jnp.where(lane == 0, ends, turn(value, 1))
 
-        def pulled(sums, x, t, dxs):
-            active = act[x, pl.ds(pl.multiple_of(8 * t + 8, 8), 8), :]
+        def pulled(sums, x, t, dxs, active):
             for dx in dxs:
                 if sums is None:
                     sums = [hats[which, 1, f, x + 1, pl.ds(8 * t + 8, 8), :] for f in range(FIELDS)]
@@ -395,7 +435,7 @@
             return sums
 
         def finish(x, t, sums):
-            own = pl.ds(pl.multiple_of(8 * t, 8), 8)
+            own = pl.ds(8 * t, 8)
             scale = inv_count[x, own, :]
             if not last:
                 scale = scale * kap[x, own, :]
@@ -403,7 +443,7 @@
                 if last:
                     result[f, x, own, :] = sums[f] * scale
                 else:
-                    w[f, x, pl.ds(pl.multiple_of(8 * t + 8, 8), 8), :] = sums[f] * scale
+                    w[f, x, pl.ds(8 * t + 8, 8), :] = sums[f] * scale
 
         def rotations(t, carry):
             padded = pl.ds(pl.multiple_of(8 * t + 8, 8), 8)
@@ -415,6 +455,16 @@
             return carry
 
         lax.fori_loop(0, TILES, rotations, 0)
+        def interior(t, carry):
+            own = pl.ds(pl.multiple_of(8 * t, 8), 8)
+            for x in range(LAYERS):
+                dxs = [dx for dx in (-1, 0, 1) if 0 <= x + dx < LAYERS]
+                sums = pulled(None, x, t, dxs, inner[x, own, :])
+                for f in range(FIELDS):
+                    acc[f, x, own, :] = sums[f]
+            return carry
+
+        lax.fori_loop(0, TILES, interior, 0)
         receive(stage, 0)
         for sy in SIGNS:
             iy = side(sy)
@@ -426,34 +476,44 @@
                     value = ry[stage, iy, p : p + 1, :]
                     hats[which, 1, f, x + 1, row : row + 1, :] = value
                     shifted(f, x + 1, slice(row, row + 1), value, placed(yz, p), lane1)
-
-        def new_ends(t, carry):
-            z = pairs(rz[stage, 1, t], rz[stage, 0, t], lane8)
-            padded = pl.ds(pl.multiple_of(8 * t + 8, 8), 8)
+        sublane = lax.broadcasted_iota(jnp.int32, (8, LANES), 0)
+        for t, row, dy in ((0, 0, -1), (TILES - 1, 7, 1)):
+            own = slice(8 * t, 8 * t + 8)
             for x in range(LAYERS):
+                active = jnp.where(sublane == row, act[x, 8 * t + 8 : 8 * t + 16, :], 0)
+                sums = [acc[f, x, own, :] for f in range(FIELDS)]
+                for dx in (-1, 0, 1):
+                    if not 0 <= x + dx < LAYERS:
+                        continue
+                    for dz in (-1, 0, 1):
+                        chosen = jnp.bitwise_and(active, 1 << offset_bit(dx, dy, dz)) != 0
+                        for f in range(FIELDS):
+                            value = hats[which, dz + 1, f, x + 1 + dx, 8 * t + 8 + dy : 8 * t + 16 + dy, :]
+                            sums[f] = sums[f] + jnp.where(chosen, value, 0.0)
                 for f in range(FIELDS):
-                    ends = placed(z, 4 * f + x)
-                    for k, lane in ((2, LANES - 1), (0, 0)):
-                        old = hats[which, k, f, x + 1, padded, :]
-                        hats[which, k, f, x + 1, padded, :] = jnp.where(lane8 == lane, ends, old)
-            return carry
-
-        lax.fori_loop(0, TILES, new_ends, 0)
-
-        def interior(t, carry):
+                    acc[f, x, own, :] = sums[f]
+        for t in range(TILES):
+            if t % 2 == 0:
+                z = pairs(rz[stage, 1, t // 2], rz[stage, 0, t // 2], lane8)
+            beyond[8 * t + 8 : 8 * t + 16, :] = turn(z, -64 * (t % 2))
+        for t in range(TILES):
+            active = ends_act[t]
+            total = zero8
+            for dy in (-1, 0, 1):
+                values = beyond[8 * t + 8 + dy : 8 * t + 16 + dy, :]
+                for dx in (-1, 0, 1):
+                    chosen = jnp.bitwise_and(active, 1 << offset_bit(dx, dy, -1)) != 0
+                    total = total + jnp.where(chosen, turn(values, -2 * dx), 0.0)
             for x in range(LAYERS):
-                if x == 0:
-                    sums = pulled(None, x, t, (0, 1))
-                elif x == LAYERS - 1:
-                    sums = pulled(None, x, t, (-1, 0))
+                sums = []
+                for f in range(FIELDS):
+                    ends = only_ends(placed(total, 4 * f + x), lane8)
+                    sums.append(acc[f, x, 8 * t : 8 * t + 8, :] + ends)
+                if x in (0, LAYERS - 1):
+                    for f in range(FIELDS):
+                        acc[f, x, 8 * t : 8 * t + 8, :] = sums[f]
                 else:
-                    finish(x, t, pulled(None, x, t, (-1, 0, 1)))
-                    continue
-                for f in range(FIELDS):
-                    acc[f, x, pl.ds(pl.multiple_of(8 * t, 8), 8), :] = sums[f]
-            return carry
-
-        lax.fori_loop(0, TILES, interior, 0)
+                    finish(x, t, sums)
         drain(stage)
         for group in range(1, 2 + CHUNKS):
             receive(stage, group)
@@ -477,7 +537,8 @@
         def boundary(t, carry):
             for x, dx in ((0, -1), (LAYERS - 1, 1)):
                 sums = [acc[f, x, pl.ds(pl.multiple_of(8 * t, 8), 8), :] for f in range(FIELDS)]
-                finish(x, t, pulled(sums, x, t, (dx,)))
+                active = act[x, pl.ds(pl.multiple_of(8 * t + 8, 8), 8), :]
+                finish(x, t, pulled(sums, x, t, (dx,), active))
             return carry
 
         lax.fori_loop(0, TILES, boundary, 0, unroll=4)
@@ -510,14 +571,14 @@
         vmem((2, 2, FIELDS + 1, ROWS, LANES), f32),
         vmem((4, 2, ROW_COUNT, LANES), f32),
         vmem((4, 4, 8, LANES), f32),
-        vmem((4, TILES, 8, LANES), f32),
+        vmem((4, TILES // 2, 8, LANES), f32),
         vmem((4, 2, 8, LANES), f32),
         vmem((4, 2, 1, LANES), f32),
         vmem((4, 4, 1, LANES), f32),
         vmem((2, 2, FIELDS + 1, ROWS, LANES), f32),
         vmem((4, 2, ROW_COUNT, LANES), f32),
         vmem((4, 4, 8, LANES), f32),
-        vmem((4, 2, TILES, 8, LANES), f32),
+        vmem((4, 2, TILES // 2, 8, LANES), f32),
         vmem((4, 2, 2, 8, LANES), f32),
         vmem((4, 2, 2, 1, LANES), f32),
         vmem((4, 4, 2, 1, LANES), f32),
@@ -525,6 +586,9 @@
         pltpu.SemaphoreType.DMA((4,)),
         pltpu.SemaphoreType.DMA((4, 2 + CHUNKS)),
         vmem((1024, 1, LANES), f32),
+        vmem(block, i32),
+        vmem((TILES, 8, LANES), i32),
+        vmem((PADDED, LANES), f32),
     ]
     in_hbm = pl.BlockSpec(memory_space=pltpu.MemorySpace.HBM)
     in_vmem = pl.BlockSpec(memory_space=pltpu.MemorySpace.VMEM)

time: 46.8 us -> 42 us (0.90)
  Pallas kernels: 45.9 us -> 41.1 us
    pallas_call x1, Pallas kernels: 45.9 us -> 41.1 us  [body(): pl.pallas_call(kernel, out_shape=jax.ShapeDtypeStruct((FIELDS,) + block,...]
where the time goes in v3:
time: 42 us; the launch traced here: 41.9 us
  Pallas kernels  41.1 us (98%)
  local copies, waits for them, and re-layouts  0.8 us (2%)
    pallas_call x1, Pallas kernels, body(): pl.pallas_call(kernel, out_shape=jax.ShapeDtypeStruct((FIELDS,) + block,...  41.1 us

profile of v3, /device:TPU:1, one launch (start us, length us, event | category | flops | bytes accessed | tf_op | source)
XLA Modules:
  0.0 41.9 jit_solution(9553511214554229061)
XLA Ops:
  0.0 41.1 %shard_map.46 = f32[4,4,64,128]{3,2,1,0:T(8,128)S(1)} custom-call(f32[4,4,64,128]{3,2,1,0:T(8,128)} %fields.1, s32[4,64,128]{2,1,0:T(8,128)} %volume_code.1, s32[4,64,128]{2,1,0:T(8,128)} %cut_flag.1, s32[4,64,128]{2,1,0:T(8,128)} %member_bits.1), custom_call_target="tpu_custom_call" | custom-call | tf_op jit(solution)/shard_map/pallas_call | solution.py:596
  41.1 0.8 %copy.6 = f32[4,4,64,128]{3,2,1,0:T(8,128)} copy(f32[4,4,64,128]{3,2,1,0:T(8,128)S(1)} %shard_map.46) | data formatting | bytes 1048576

commit v4 on v3

--- a/solution.py
+++ b/solution.py
@@ -12,9 +12,9 @@
 TILES = ROWS // 8
 PADDED = ROWS + 16
 LANES = 128
-CHUNK = 16
+CHUNK = 8
 CHUNKS = ROWS // CHUNK
-ORDER = (0, CHUNKS - 1) + tuple(range(1, CHUNKS - 1))
+ORDER = (1, 2, 0, CHUNKS - 1) + tuple(range(3, CHUNKS - 1))
 ROW_COUNT = 24
 SIGNS = (-1, 1)
 
@@ -135,7 +135,7 @@
             source, target = yzpack.at[stage, iy], ryz.at[stage, iy, iz]
         else:
             source, target = cpack.at[stage, e], rc.at[stage, e, iz]
-        group = 0 if sx == 0 else 1 if sy or sz else 2 + chunk
+        group = 0 if sx == 0 else 1 if sy else 2 if sz else 3 + chunk
         return pltpu.make_async_remote_copy(
             src_ref=source,
             dst_ref=target,
@@ -165,7 +165,7 @@
         pltpu.make_async_copy(part, part, semaphore).wait()
 
     def receive(stage, group):
-        chosen = [beside, small, None][min(group, 2)] or faces((group - 2,))
+        chosen = [beside, corner, column, None][min(group, 3)] or faces((group - 3,))
         rows = sum(rows_of(stage, which) for which in MESSAGES if chosen(*which))
         await_rows(recv_sem.at[stage, group], rows)
 
@@ -175,8 +175,11 @@
     def beside(sx, sy, sz, chunk):
         return sx == 0
 
-    def small(sx, sy, sz, chunk):
-        return sx != 0 and (sy != 0 or sz != 0)
+    def corner(sx, sy, sz, chunk):
+        return sx != 0 and sy != 0
+
+    def column(sx, sy, sz, chunk):
+        return sx != 0 and sy == 0 and sz != 0
 
     def faces(wanted):
         return lambda sx, sy, sz, chunk: sx != 0 and sy == 0 and sz == 0 and chunk in wanted
@@ -242,8 +245,7 @@
         ends_act[t] = jnp.bitwise_and(wide, jnp.bitwise_not(beyond_x | beyond_y))
         return carry
 
-    def scatter(stage, count):
-        which = stage // 2
+    def scatter_edges(stage, count):
         for sx in SIGNS:
             xt = -1 if sx == -1 else LAYERS
             ix = side(sx)
@@ -259,6 +261,9 @@
         if stage == 0:
             pl.semaphore_wait(barrier, len(TRAVEL))
         send(stage, lambda sx, sy, sz, chunk: sx != 0 and sy != 0)
+
+    def scatter(stage, count):
+        which = stage // 2
         for sx in SIGNS:
             xt = -1 if sx == -1 else LAYERS
             ix = side(sx)
@@ -284,9 +289,6 @@
                     pack = packed(pack, ends[f], p, lane8)
             yzpack[stage, side(sy)] = pack[row : row + 1, :]
         send(stage, lambda sx, sy, sz, chunk: sx == 0 and sy != 0)
-        if stage == 0:
-            lax.fori_loop(0, TILES, split_bits, 0)
-
         def rest(pair, carry):
             pack = zero8
             for half in range(2):
@@ -302,6 +304,8 @@
 
         lax.fori_loop(0, TILES // 2, rest, 0)
         send(stage, lambda sx, sy, sz, chunk: (sx, sy) == (0, 0))
+        if stage == 0:
+            lax.fori_loop(0, TILES, split_bits, 0)
 
     def combine(stage, count):
         odd = stage + 1
@@ -327,20 +331,23 @@
                     p = 4 * f + x
                     value = ry[stage, iy, p : p + 1, :] + only_ends(placed(yz, p), lane1)
                     acc[f, x, row : row + 1, :] += value
-        for t in range(TILES):
-            if t % 2 == 0:
-                z = pairs(rz[stage, 1, t // 2], rz[stage, 0, t // 2], lane8)
-            for x in range(LAYERS):
-                sums = []
-                for f in range(count):
-                    value = acc[f, x, 8 * t : 8 * t + 8, :] + only_ends(placed(z, 4 * f + x + 32 * (t % 2)), lane8)
-                    sums.append(value)
-                if x in (0, LAYERS - 1):
+        def z_ends(layers):
+            for t in range(TILES):
+                if t % 2 == 0:
+                    z = pairs(rz[stage, 1, t // 2], rz[stage, 0, t // 2], lane8)
+                for x in layers:
+                    sums = []
                     for f in range(count):
-                        acc[f, x, 8 * t : 8 * t + 8, :] = sums[f]
-                else:
-                    finish(x, t, sums)
-        receive(stage, 1)
+                        ends = only_ends(placed(z, 4 * f + x + 32 * (t % 2)), lane8)
+                        sums.append(acc[f, x, 8 * t : 8 * t + 8, :] + ends)
+                    if x in (0, LAYERS - 1):
+                        for f in range(count):
+                            acc[f, x, 8 * t : 8 * t + 8, :] = sums[f]
+                    else:
+                        finish(x, t, sums)
+
+        z_ends((0, LAYERS - 1))
+        receive(stage, 2)
         for sx in SIGNS:
             ix = side(sx)
             x = 0 if sx == 1 else LAYERS - 1
@@ -348,16 +355,25 @@
             for t in range(TILES):
                 for f in range(count):
                     acc[f, x, 8 * t : 8 * t + 8, :] += only_ends(placed(xz, count * t + f), lane8)
-            for sy in SIGNS:
-                e = 2 * ix + side(sy)
-                row = 0 if sy == 1 else ROWS - 1
-                corner = pairs(rc[stage, e, 1], rc[stage, e, 0], lane1)
-                for f in range(count):
-                    value = re[stage, e, f : f + 1, :] + only_ends(placed(corner, f), lane1)
-                    acc[f, x, row : row + 1, :] += value
+
+        def corner_rows():
+            receive(stage, 1)
+            for sx in SIGNS:
+                ix = side(sx)
+                x = 0 if sx == 1 else LAYERS - 1
+                for sy in SIGNS:
+                    e = 2 * ix + side(sy)
+                    row = 0 if sy == 1 else ROWS - 1
+                    corner = pairs(rc[stage, e, 1], rc[stage, e, 0], lane1)
+                    for f in range(count):
+                        value = re[stage, e, f : f + 1, :] + only_ends(placed(corner, f), lane1)
+                        acc[f, x, row : row + 1, :] += value
+
         for position, chunk in enumerate(ORDER):
-            receive(stage, 2 + chunk)
-            for t in range(chunk * CHUNK // 8, (chunk + 1) * CHUNK // 8):
+            if chunk == 0:
+                corner_rows()
+            receive(stage, 3 + chunk)
+            for t in (chunk,):
                 for sx in SIGNS:
                     x = 0 if sx == 1 else LAYERS - 1
                     sums = []
@@ -365,7 +381,7 @@
                         own = slice(8 * t, 8 * t + 8)
                         sums.append(acc[f, x, own, :] + rx[which, side(sx), f, own, :])
                     finish(x, t, sums)
-            if position == 1:
+            if position == 3:
                 for sx in SIGNS:
                     x = 0 if sx == -1 else LAYERS - 1
                     for sy in SIGNS:
@@ -378,6 +394,7 @@
                             pack = packed(pack, value, f, lane1)
                         cpack[odd, e] = pack
                 send(odd, lambda sx, sy, sz, chunk: sx != 0 and sy != 0)
+                send(odd, faces((chunk,)))
                 for sy in SIGNS:
                     row = 8 if sy == -1 else 7 + ROWS
                     pack = jnp.zeros((1, LANES), jnp.float32)
@@ -399,7 +416,10 @@
                             pack = packed(pack, value, FIELDS * t + f, lane8)
                     xzpack[odd, side(sx)] = pack
                 send(odd, lambda sx, sy, sz, chunk: sx != 0 and sy == 0 and sz != 0)
-            send(odd, faces((chunk,)))
+            if position != 3:
+                send(odd, faces((chunk,)))
+            if position < 2:
+                z_ends((position + 1,))
         for pair in range(TILES // 2):
             pack = zero8
             for t in (2 * pair, 2 * pair + 1):
@@ -409,9 +429,8 @@
                         pack = packed(pack, value, 4 * f + x + 32 * (t % 2), lane8)
             zpack[odd, pair] = pack
         send(odd, lambda sx, sy, sz, chunk: (sx, sy) == (0, 0))
-        drain(stage)
-
-    def gather(stage, last):
+
+    def gather(stage, last, between):
         which = stage // 2
 
         def shifted(f, xi, rows, value, ends, lane):
@@ -514,8 +533,8 @@
                         acc[f, x, 8 * t : 8 * t + 8, :] = sums[f]
                 else:
                     finish(x, t, sums)
-        drain(stage)
-        for group in range(1, 2 + CHUNKS):
+        drain(stage - 1)
+        for group in range(1, 3 + CHUNKS):
             receive(stage, group)
         for sx in SIGNS:
             ix = side(sx)
@@ -536,19 +555,25 @@
 
         def boundary(t, carry):
             for x, dx in ((0, -1), (LAYERS - 1, 1)):
-                sums = [acc[f, x, pl.ds(pl.multiple_of(8 * t, 8), 8), :] for f in range(FIELDS)]
-                active = act[x, pl.ds(pl.multiple_of(8 * t + 8, 8), 8), :]
+                sums = [acc[f, x, pl.ds(8 * t, 8), :] for f in range(FIELDS)]
+                active = act[x, pl.ds(8 * t + 8, 8), :]
                 finish(x, t, pulled(sums, x, t, (dx,), active))
             return carry
 
-        lax.fori_loop(0, TILES, boundary, 0, unroll=4)
-
+        boundary(0, 0)
+        boundary(TILES - 1, 0)
+        between()
+        lax.fori_loop(1, TILES - 1, boundary, 0, unroll=3)
+
+    scatter_edges(0, FIELDS + 1)
     scatter(0, FIELDS + 1)
     combine(0, FIELDS + 1)
-    gather(1, False)
+    gather(1, False, lambda: scatter_edges(2, FIELDS))
     scatter(2, FIELDS)
     combine(2, FIELDS)
-    gather(3, True)
+    gather(3, True, lambda: None)
+    drain(1)
+    drain(3)
 
 
 def body(fields, volume_code, cut_flag, member_bits):
@@ -584,7 +609,7 @@
         vmem((4, 4, 2, 1, LANES), f32),
         pltpu.SemaphoreType.DMA((4,)),
         pltpu.SemaphoreType.DMA((4,)),
-        pltpu.SemaphoreType.DMA((4, 2 + CHUNKS)),
+        pltpu.SemaphoreType.DMA((4, 3 + CHUNKS)),
         vmem((1024, 1, LANES), f32),
         vmem(block, i32),
         vmem((TILES, 8, LANES), i32),

time: 42 us -> 41.6 us (level)
    pallas_call x1, Pallas kernels: 41.1 us -> 40.7 us  [body(): pl.pallas_call(kernel, out_shape=jax.ShapeDtypeStruct((FIELDS,) + block,...]
where the time goes in v4:
time: 41.6 us; the launch traced here: 41.5 us
  Pallas kernels  40.7 us (98%)
  local copies, waits for them, and re-layouts  0.8 us (2%)
    pallas_call x1, Pallas kernels, body(): pl.pallas_call(kernel, out_shape=jax.ShapeDtypeStruct((FIELDS,) + block,...  40.7 us

profile of v4, /device:TPU:1, one launch (start us, length us, event | category | flops | bytes accessed | tf_op | source)
XLA Modules:
  0.0 41.5 jit_solution(5241179232435422205)
XLA Ops:
  0.0 40.7 %shard_map.46 = f32[4,4,64,128]{3,2,1,0:T(8,128)S(1)} custom-call(f32[4,4,64,128]{3,2,1,0:T(8,128)} %fields.1, s32[4,64,128]{2,1,0:T(8,128)} %volume_code.1, s32[4,64,128]{2,1,0:T(8,128)} %cut_flag.1, s32[4,64,128]{2,1,0:T(8,128)} %member_bits.1), custom_call_target="tpu_custom_call" | custom-call | tf_op jit(solution)/shard_map/pallas_call | solution.py:621
  40.7 0.8 %copy.6 = f32[4,4,64,128]{3,2,1,0:T(8,128)} copy(f32[4,4,64,128]{3,2,1,0:T(8,128)S(1)} %shard_map.46) | data formatting | bytes 1048576
